TPU v7x, 32 devices: a whole 2x2x4 slice. The times are simulated.
32 devices in a mesh: freq: 4 (over z), trace: 8 (over y, x, core).
Axes of the slice: x: 2, y: 2, z: 4, core: 2. Of those that a mesh axis runs over, the one named last changes fastest.
Arguments:
- recorded: float32 [8, 2, 2048, 1024], P(None, None, 'freq', 'trace'), may hold values from -16 to 16
- multiples: float32 [8, 2, 2048, 1024], P(None, None, 'freq', 'trace'), may hold values from -6 to 6
Outputs:
- primaries: float32 [8, 2, 2048, 1024], P(None, None, 'freq', 'trace')
- filters: float32 [8, 2, 32, 64], P(None, None, 'freq')
All inputs are finite; a program needn't handle non-finite values.
Results may differ from a plain program's by a relative error of at most 0.0001.
Values sent between devices are 32-bit elements; how exact they have to be, the bound alone decides.
A program may use at most 128 MiB of HBM per device.

v0:
```python
import jax
import jax.numpy as jnp
from jax import lax
from jax.sharding import PartitionSpec as P

FB = 64
TAPS = 64
ITERS = 3


def with_halo(value, sides, width):
    for axis, dim in sides:
        size, length = (lax.axis_size(axis), value.shape[dim])
        up = [(i, (i + 1) % size) for i in range(size - 1)]
        down = [(j, i) for i, j in up]
        last = lax.slice_in_dim(value, length - width, length, axis=dim)
        first = lax.slice_in_dim(value, 0, width, axis=dim)
        before = lax.ppermute(last, axis, up)
        after = lax.ppermute(first, axis, down)
        value = jnp.concatenate([before, value, after], axis=dim)
    return value


def toeplitz_rows(taps_vec, trace_rows):
    tap_count = taps_vec.shape[-1]
    window_len = trace_rows + tap_count
    leading = taps_vec.shape[:-1]
    padded = jnp.concatenate(
        [
            jnp.zeros(leading + (1,), jnp.float32),
            taps_vec[..., ::-1],
            jnp.zeros(leading + (trace_rows,), jnp.float32),
        ],
        -1,
    )
    repeated = jnp.tile(padded, (1,) * len(leading) + (trace_rows,))
    return repeated[..., : trace_rows * window_len].reshape(leading + (trace_rows, window_len))


def product(left, right):
    return jnp.einsum("bfj,bxj->bfx", left, right, precision=lax.Precision.HIGHEST)


def correlate(left, right):
    return jnp.einsum("bfj,bfx->bxj", left, right, precision=lax.Precision.HIGHEST)


def forward_one(window, taps_vec):
    trace_rows = window.shape[-1] - taps_vec.shape[-1]
    toeplitz = toeplitz_rows(taps_vec, trace_rows)
    real_part = product(window[0], toeplitz[0]) - product(window[1], toeplitz[1])
    imag_part = product(window[0], toeplitz[1]) + product(window[1], toeplitz[0])
    return jnp.stack([real_part, imag_part])


def adjoint_one(window, residual, tap_count):
    real_part = correlate(window[0], residual[0]) + correlate(window[1], residual[1])
    imag_part = correlate(window[0], residual[1]) - correlate(window[1], residual[0])
    crossed = jnp.stack([real_part, imag_part])
    trace_rows, window_len = crossed.shape[-2:]
    leading = crossed.shape[:-2]
    flattened = crossed.reshape(leading + (trace_rows * window_len,))
    flattened = jnp.concatenate([flattened, jnp.zeros(leading + (trace_rows,), jnp.float32)], -1)
    column_sums = jnp.sum(flattened.reshape(leading + (trace_rows, window_len + 1)), axis=-2)
    return column_sums[..., 1 : tap_count + 1][..., ::-1]


def bending(edge_pad):
    return 2.0 * edge_pad[:, :, 1:-1] - edge_pad[:, :, :-2] - edge_pad[:, :, 2:]


def inner_sum(left, right):
    return jnp.sum(left * right, axis=(1, 2, 3))


def body(recorded, multiples):
    half_taps = TAPS // 2
    trace_rows = multiples.shape[3]
    edged = with_halo(multiples, (("trace", 3),), half_taps)
    shot_count, part_count, freq_rows, window_len = edged.shape
    block_count = freq_rows // FB
    windows = edged.reshape(shot_count, part_count, block_count, FB, window_len)
    trace_count = lax.axis_size("trace")
    weight = 0.5 * FB * trace_rows * trace_count
    residual = recorded
    shaping = jnp.zeros((shot_count, part_count, block_count, TAPS), jnp.float32)
    bent_sum = jnp.zeros_like(shaping)
    direction = shaping
    norm_now = jnp.ones((shot_count,), jnp.float32)
    for iteration in range(ITERS):
        pieces = residual.reshape(shot_count, part_count, block_count, FB, trace_rows)
        gradient = (
            lax.psum(
                lax.map(lambda paired: adjoint_one(paired[0], paired[1], TAPS), (windows, pieces)),
                "trace",
            )
            - bent_sum
        )
        norm_next = lax.psum(inner_sum(gradient, gradient), "freq")
        if iteration == 0:
            direction = gradient
        else:
            direction = gradient + (norm_next / norm_now)[:, None, None, None] * direction
        norm_now = norm_next
        result = lax.map(lambda paired: forward_one(paired[0], paired[1]), (windows, direction))
        applied = result.reshape(shot_count, part_count, freq_rows, trace_rows)
        edge_pad = with_halo(direction, (("freq", 2),), 1)
        smooth = weight * bending(edge_pad)
        energy_sum, smooth_sum = lax.psum(
            (jnp.sum(applied * applied, axis=(1, 2, 3)), inner_sum(direction, smooth)),
            ("freq", "trace"),
        )
        energy = energy_sum + smooth_sum / trace_count
        step_len = (norm_now / energy)[:, None, None, None]
        shaping = shaping + step_len * direction
        residual = residual - step_len * applied
        bent_sum = bent_sum + step_len * smooth
    return (residual, shaping)


def solution(mesh):
    return jax.shard_map(
        body,
        mesh=mesh,
        in_specs=(P(None, None, "freq", "trace"), P(None, None, "freq", "trace")),
        out_specs=(P(None, None, "freq", "trace"), P(None, None, "freq", None)),
        check_vma=False,
    )
```

profile of v0, /device:TPU:0, one launch (start us, length us, event | category | flops | bytes accessed | tf_op | source)
XLA Modules:
  0.0 1106.0 jit_solution(16259001931993445002)
XLA Ops:
  0.6 8.0 fusion.60
  27.1 8.8 pad_maximum_fusion
  35.8 140.7 %while.60 = (s32[]{:T(128)}, f32[8,2,8,64]{3,2,1,0:T(8,128)S(1)}, f32[8,2,8,64,128]{4,3,2,1,0:T(8,128)}, f32[8,2,8,64,192]{4,3,2,1,0:T(8,128)}, s32[]{:T(128)}, /*index=5*/s32[]{:T(128)}, s32[]{}, f32[]{:T(128)}) while((s32[]{:T(128)}, f32[8,2,8,64]{3,2,1,0:T(8,128)S(1)}, f32[8,2,8,64,128]{4,3,2,1,0:T(8,128)}, ...), condition=%wide.region_2.3_spmd, body=%wide.region_0.2_spmd.sunk | while | flops 606346240 | bytes 22103216 | solution.py:94
  48.9 4.2 reshape.130
  66.4 4.2 reshape.130
  84.0 4.2 reshape.130
  101.6 4.2 reshape.130
  119.2 4.2 reshape.130
  154.3 4.2 reshape.130
  171.9 4.2 reshape.130
  176.5 40.3 %psum.84 = f32[8,2,8,64]{3,2,1,0:T(8,128)S(1)} all-reduce(f32[8,2,8,64]{3,2,1,0:T(8,128)S(1)} %get-tuple-element.134), channel_id=1, replica_groups=mesh['freq'=4,'trace'=8] {'trace'}, use_global_device_ids=true, to_apply=%region_3.4 | all-reduce | flops 8192 | bytes 65536 | tf_op jit(solution)/shard_map/psum | solution.py:93
  224.4 120.3 %while.61 = (s32[]{:T(128)}, f32[8,2,8,64,128]{4,3,2,1,0:T(8,128)}, f32[8,2,8,64,192]{4,3,2,1,0:T(8,128)}, f32[8,2,8,64]{3,2,1,0:T(8,128)S(1)}, s32[]{:T(128)}, /*index=5*/f32[]{:T(128)}, f32[]{:T(128)}, s32[]{:T(128)}, s32[]{}) while((s32[]{:T(128)}, f32[8,2,8,64,128]{4,3,2,1,0:T(8,128)}, f32[8,2,8,64,192]{4,3,2,1,0:T(8,128)}, ...), condition=%wide.region_7.8_spmd, body=%wide.region_6.7_spmd.sunk | while | flops 604248064 | bytes 18950932 | solution.py:105
  347.5 13.0 %psum.85 = f32[8]{0:T(128)S(1)} all-reduce(f32[8]{0:T(128)S(1)} %get-tuple-element.141), channel_id=1, replica_groups=mesh['freq'=4,'trace'=8] {'freq'}, use_global_device_ids=true, to_apply=%region_5.6 | all-reduce | flops 8 | bytes 64 | tf_op jit(solution)/shard_map/psum | solution.py:99
  360.5 37.8 %all-reduce.5 = (f32[8]{0:T(128)S(1)}, f32[8]{0:T(128)S(1)}) all-reduce(f32[8]{0:T(128)S(1)} %multiply_reduce_fusion.2, f32[8]{0:T(128)S(1)} %get-tuple-element.140), channel_id=1, replica_groups=mesh['freq'=4,'trace'=8] {'freq','trace'}, use_global_device_ids=true, to_apply=%region_9.10 | all-reduce | flops 16 | bytes 128 | tf_op jit(solution)/shard_map/psum | solution.py:109
  398.3 6.0 fusion.47
  404.3 140.6 %while.62 = (s32[]{:T(128)}, f32[8,2,8,64]{3,2,1,0:T(8,128)S(1)}, f32[8,2,8,64,128]{4,3,2,1,0:T(8,128)}, f32[8,2,8,64,192]{4,3,2,1,0:T(8,128)}, s32[]{:T(128)}, /*index=5*/s32[]{:T(128)}, s32[]{}, f32[]{:T(128)}) while((s32[]{:T(128)}, f32[8,2,8,64]{3,2,1,0:T(8,128)S(1)}, f32[8,2,8,64,128]{4,3,2,1,0:T(8,128)}, ...), condition=%wide.region_14.15_spmd, body=%wide.region_12.14_spmd.sunk | while | flops 606346240 | bytes 22103216 | solution.py:94
  434.9 4.2 reshape.131
  452.5 4.2 reshape.131
  487.6 4.2 reshape.131
  505.2 4.2 reshape.131
  540.4 4.2 reshape.131
  544.9 23.8 %psum.88 = f32[8,2,8,64]{3,2,1,0:T(8,128)S(1)} all-reduce(f32[8,2,8,64]{3,2,1,0:T(8,128)S(1)} %get-tuple-element.136), channel_id=1, replica_groups=mesh['freq'=4,'trace'=8] {'trace'}, use_global_device_ids=true, to_apply=%region_15.16 | all-reduce | flops 8192 | bytes 65536 | tf_op jit(solution)/shard_map/psum | solution.py:93
  569.0 11.2 %psum.89 = f32[8]{0:T(128)S(1)} all-reduce(f32[8]{0:T(128)S(1)} %multiply_reduce_fusion.5), channel_id=1, replica_groups=mesh['freq'=4,'trace'=8] {'freq'}, use_global_device_ids=true, to_apply=%region_17.18 | all-reduce | flops 8 | bytes 64 | tf_op jit(solution)/shard_map/psum | solution.py:99
  585.9 120.0 %while.63 = (s32[]{:T(128)}, f32[8,2,8,64,128]{4,3,2,1,0:T(8,128)}, f32[8,2,8,64,192]{4,3,2,1,0:T(8,128)}, f32[8,2,8,64]{3,2,1,0:T(8,128)S(1)}, s32[]{:T(128)}, /*index=5*/f32[]{:T(128)}, f32[]{:T(128)}, s32[]{:T(128)}, s32[]{}) while((s32[]{:T(128)}, f32[8,2,8,64,128]{4,3,2,1,0:T(8,128)}, f32[8,2,8,64,192]{4,3,2,1,0:T(8,128)}, ...), condition=%wide.region_19.20_spmd, body=%wide.region_18.19_spmd.sunk | while | flops 604248064 | bytes 18950932 | solution.py:105
  708.8 40.5 %all-reduce.4 = (f32[8]{0:T(128)S(1)}, f32[8]{0:T(128)S(1)}) all-reduce(f32[8]{0:T(128)S(1)} %multiply_reduce_fusion.1, f32[8]{0:T(128)S(1)} %multiply_reduce_fusion.4), channel_id=1, replica_groups=mesh['freq'=4,'trace'=8] {'freq','trace'}, use_global_device_ids=true, to_apply=%region_21.22 | all-reduce | flops 16 | bytes 128 | tf_op jit(solution)/shard_map/psum | solution.py:109
  749.3 6.0 fusion.46
  755.3 140.6 %while.64 = (s32[]{:T(128)}, f32[8,2,8,64]{3,2,1,0:T(8,128)S(1)}, f32[8,2,8,64,128]{4,3,2,1,0:T(8,128)}, f32[8,2,8,64,192]{4,3,2,1,0:T(8,128)}, s32[]{:T(128)}, /*index=5*/s32[]{:T(128)}, s32[]{}, f32[]{:T(128)}) while((s32[]{:T(128)}, f32[8,2,8,64]{3,2,1,0:T(8,128)S(1)}, f32[8,2,8,64,128]{4,3,2,1,0:T(8,128)}, ...), condition=%wide.region_26.27_spmd, body=%wide.region_24.26_spmd.sunk | while | flops 606346240 | bytes 22103216 | solution.py:94
  896.0 23.5 %psum.92 = f32[8,2,8,64]{3,2,1,0:T(8,128)S(1)} all-reduce(f32[8,2,8,64]{3,2,1,0:T(8,128)S(1)} %get-tuple-element.138), channel_id=1, replica_groups=mesh['freq'=4,'trace'=8] {'trace'}, use_global_device_ids=true, to_apply=%region_27.28 | all-reduce | flops 8192 | bytes 65536 | tf_op jit(solution)/shard_map/psum | solution.py:93
  919.7 9.9 psum.93
  936.1 119.7 %while.65 = (s32[]{:T(128)}, f32[8,2,8,64,128]{4,3,2,1,0:T(8,128)}, f32[8,2,8,64,192]{4,3,2,1,0:T(8,128)}, f32[8,2,8,64]{3,2,1,0:T(8,128)S(1)}, s32[]{:T(128)}, /*index=5*/f32[]{:T(128)}, f32[]{:T(128)}, s32[]{:T(128)}, s32[]{}) while((s32[]{:T(128)}, f32[8,2,8,64,128]{4,3,2,1,0:T(8,128)}, f32[8,2,8,64,192]{4,3,2,1,0:T(8,128)}, ...), condition=%wide.region_31.32_spmd, body=%wide.region_30.31_spmd.sunk | while | flops 604248064 | bytes 18950932 | solution.py:105
  1058.7 40.3 %all-reduce.3 = (f32[8]{0:T(128)S(1)}, f32[8]{0:T(128)S(1)}) all-reduce(f32[8]{0:T(128)S(1)} %multiply_reduce_fusion, f32[8]{0:T(128)S(1)} %fusion.51), channel_id=1, replica_groups=mesh['freq'=4,'trace'=8] {'freq','trace'}, use_global_device_ids=true, to_apply=%region_33.34 | all-reduce | flops 16 | bytes 128 | tf_op jit(solution)/shard_map/psum | solution.py:109
  1099.7 6.1 fusion.45
  (753 shorter events, 775.5 us)
Async XLA Ops:
  11.4 6.8 collective-permute-start
  16.7 6.7 collective-permute-start.1
  216.9 130.4 %collective-permute-start.2 = (f32[8,2,1,64]{3,2,1,0:T(1,128)S(1)}, f32[8,2,1,64]{3,2,1,0:T(1,128)S(1)}, u32[]{:S(2)}, u32[]{:S(2)}) collective-permute-start(f32[8,2,1,64]{3,2,1,0:T(1,128)S(1)} %get-tuple-element.214), channel_id=1, source_target_pairs={{0,8},{8,16},{16,24},{1,9},{9,17},{17,25},{2,10},{10,18},{18,26},{... | collective-permute-start | bytes 12296 | tf_op jit(solution)/shard_map/ppermute | solution.py:18
  220.3 126.9 %collective-permute-start.3 = (f32[8,2,1,64]{3,2,1,0:T(1,128)S(1)}, f32[8,2,1,64]{3,2,1,0:T(1,128)S(1)}, u32[]{:S(2)}, u32[]{:S(2)}) collective-permute-start(f32[8,2,1,64]{3,2,1,0:T(1,128)S(1)} %get-tuple-element.215), channel_id=1, source_target_pairs={{8,0},{16,8},{24,16},{9,1},{17,9},{25,17},{10,2},{18,10},{26,18},{... | collective-permute-start | bytes 12296 | tf_op jit(solution)/shard_map/ppermute | solution.py:19
  580.3 128.3 %collective-permute-start.4 = (f32[8,2,1,64]{3,2,1,0:T(1,128)S(1)}, f32[8,2,1,64]{3,2,1,0:T(1,128)S(1)}, u32[]{:S(2)}, u32[]{:S(2)}) collective-permute-start(f32[8,2,1,64]{3,2,1,0:T(1,128)S(1)} %get-tuple-element.212), channel_id=1, source_target_pairs={{0,8},{8,16},{16,24},{1,9},{9,17},{17,25},{2,10},{10,18},{18,26},{... | collective-permute-start | bytes 12296 | tf_op jit(solution)/shard_map/ppermute | solution.py:18
  581.9 126.7 %collective-permute-start.5 = (f32[8,2,1,64]{3,2,1,0:T(1,128)S(1)}, f32[8,2,1,64]{3,2,1,0:T(1,128)S(1)}, u32[]{:S(2)}, u32[]{:S(2)}) collective-permute-start(f32[8,2,1,64]{3,2,1,0:T(1,128)S(1)} %get-tuple-element.213), channel_id=1, source_target_pairs={{8,0},{16,8},{24,16},{9,1},{17,9},{25,17},{10,2},{18,10},{26,18},{... | collective-permute-start | bytes 12296 | tf_op jit(solution)/shard_map/ppermute | solution.py:19
  929.8 128.7 %collective-permute-start.6 = (f32[8,2,1,64]{3,2,1,0:T(1,128)S(1)}, f32[8,2,1,64]{3,2,1,0:T(1,128)S(1)}, u32[]{:S(2)}, u32[]{:S(2)}) collective-permute-start(f32[8,2,1,64]{3,2,1,0:T(1,128)S(1)} %get-tuple-element.210), channel_id=1, source_target_pairs={{0,8},{8,16},{16,24},{1,9},{9,17},{17,25},{2,10},{10,18},{18,26},{... | collective-permute-start | bytes 12296 | tf_op jit(solution)/shard_map/ppermute | solution.py:18
  932.1 126.4 %collective-permute-start.7 = (f32[8,2,1,64]{3,2,1,0:T(1,128)S(1)}, f32[8,2,1,64]{3,2,1,0:T(1,128)S(1)}, u32[]{:S(2)}, u32[]{:S(2)}) collective-permute-start(f32[8,2,1,64]{3,2,1,0:T(1,128)S(1)} %get-tuple-element.211), channel_id=1, source_target_pairs={{8,0},{16,8},{24,16},{9,1},{17,9},{25,17},{10,2},{18,10},{26,18},{... | collective-permute-start | bytes 12296 | tf_op jit(solution)/shard_map/ppermute | solution.py:19
where the time goes:
time: 1120 us; the launch traced here: 1110 us
  matrix products  463 us (41%)
  local copies, waits for them, and re-layouts  287 us (26%)
  blocking collectives  240 us (21%)
  other arithmetic  93.1 us (8%)
  starting transfers between devices  15.8 us (1%)
    dot_general x96, matrix products, correlate(): jnp.einsum('bfj,bfx->bxj', left, right, precision=lax.Precision.HIGHEST)  246 us
    dot_general x96, matrix products, product(): jnp.einsum('bfj,bxj->bfx', left, right, precision=lax.Precision.HIGHEST)  217 us
    psum x3, blocking collectives, body(): lax.psum((jnp.sum(applied * applied, axis=(1, 2, 3)), inner_sum(direction...  119 us
    reshape x24, local copies, waits for them, and re-layouts, adjoint_one(): flattened.reshape(leading + (trace_rows, window_len + 1))  102 us
    psum x3, blocking collectives, body(): lax.psum(lax.map(lambda paired: adjoint_one(paired[0], paired[1], TAPS),...  87.7 us
    another operation x48, local copies, waits for them, and re-layouts, toeplitz_rows(): repeated = jnp.tile(padded, (1,) * len(leading) + (trace_rows,))  57.1 us
    slice x24, local copies, waits for them, and re-layouts, forward_one(): toeplitz[0]  35.3 us
    psum x3, blocking collectives, body(): norm_next = lax.psum(inner_sum(gradient, gradient), 'freq')  34.1 us
  transfers between devices with their start and end apart: 8, of which 1 were waited for; matrix products, arithmetic and copies ran while one was open for 34% of the time, Pallas kernels for 0%

commit v1 on v0

--- a/solution.py
+++ b/solution.py
@@ -89,10 +89,14 @@
     norm_now = jnp.ones((shot_count,), jnp.float32)
     for iteration in range(ITERS):
         pieces = residual.reshape(shot_count, part_count, block_count, FB, trace_rows)
+
+        def _detail_lines(local_array):
+            y_new = jnp.sum(lax.all_gather(local_array, axis_name="trace"), axis=0)
+            return y_new
+
         gradient = (
-            lax.psum(
-                lax.map(lambda paired: adjoint_one(paired[0], paired[1], TAPS), (windows, pieces)),
-                "trace",
+            _detail_lines(
+                lax.map(lambda paired: adjoint_one(paired[0], paired[1], TAPS), (windows, pieces))
             )
             - bent_sum
         )

time: 1120 us -> 1080 us (0.964)
  blocking collectives: 240 us -> 200 us
    psum x3 -> x0, blocking collectives: 87.7 us -> none  [body(): lax.psum(lax.map(lambda paired: adjoint_one(paired[0], paired[1], TAPS),...]
    all_gather x0 -> x3, blocking collectives: none -> 47.8 us  [_detail_lines(): y_new = jnp.sum(lax.all_gather(local_array, axis_name='trace'), axis=0)]
  transfers between devices with their start and end apart: 8 -> 8, of which waited for: 1 -> 1; matrix products, arithmetic and copies ran while one was open for 34% -> 36% of each run, Pallas kernels for 0% -> 0%
where the time goes in v1:
time: 1080 us; the launch traced here: 1070 us
  matrix products  463 us (43%)
  local copies, waits for them, and re-layouts  287 us (27%)
  blocking collectives  200 us (19%)
  other arithmetic  93.2 us (9%)
  starting transfers between devices  15.6 us (1%)
    dot_general x96, matrix products, correlate(): jnp.einsum('bfj,bfx->bxj', left, right, precision=lax.Precision.HIGHEST)  246 us
    dot_general x96, matrix products, product(): jnp.einsum('bfj,bxj->bfx', left, right, precision=lax.Precision.HIGHEST)  217 us
    psum x3, blocking collectives, body(): lax.psum((jnp.sum(applied * applied, axis=(1, 2, 3)), inner_sum(direction...  118 us
    reshape x24, local copies, waits for them, and re-layouts, adjoint_one(): flattened.reshape(leading + (trace_rows, window_len + 1))  102 us
    another operation x48, local copies, waits for them, and re-layouts, toeplitz_rows(): repeated = jnp.tile(padded, (1,) * len(leading) + (trace_rows,))  57.1 us
    all_gather x3, blocking collectives, _detail_lines(): y_new = jnp.sum(lax.all_gather(local_array, axis_name='trace'), axis=0)  47.8 us
    slice x24, local copies, waits for them, and re-layouts, forward_one(): toeplitz[0]  35.3 us
    psum x3, blocking collectives, body(): norm_next = lax.psum(inner_sum(gradient, gradient), 'freq')  34.2 us
  transfers between devices with their start and end apart: 8, of which 1 were waited for; matrix products, arithmetic and copies ran while one was open for 36% of the time, Pallas kernels for 0%

profile of v1, /device:TPU:0, one launch (start us, length us, event | category | flops | bytes accessed | tf_op | source)
XLA Modules:
  0.0 1065.5 jit_solution(9114947246544598918)
XLA Ops:
  0.6 8.0 fusion.60
  27.1 8.8 pad_maximum_fusion
  35.8 140.7 %while.60 = (s32[]{:T(128)}, f32[8,2,8,64]{3,2,1,0:T(8,128)S(1)}, f32[8,2,8,64,128]{4,3,2,1,0:T(8,128)}, f32[8,2,8,64,192]{4,3,2,1,0:T(8,128)}, s32[]{:T(128)}, /*index=5*/s32[]{:T(128)}, s32[]{}, f32[]{:T(128)}) while((s32[]{:T(128)}, f32[8,2,8,64]{3,2,1,0:T(8,128)S(1)}, f32[8,2,8,64,128]{4,3,2,1,0:T(8,128)}, ...), condition=%wide.region_2.3_spmd, body=%wide.region_0.2_spmd.sunk | while | flops 606346240 | bytes 22103216 | solution.py:99
  48.9 4.2 reshape.133
  66.4 4.2 reshape.133
  84.0 4.2 reshape.133
  101.6 4.2 reshape.133
  119.2 4.2 reshape.133
  154.3 4.2 reshape.133
  171.9 4.2 reshape.133
  176.5 26.6 %all-gather = f32[64,2,8,64]{3,2,1,0:T(8,128)S(1)} all-gather(f32[8,2,8,64]{3,2,1,0:T(8,128)S(1)} %get-tuple-element.134), channel_id=2, replica_groups=mesh['freq'=4,'trace'=8] {'trace'}, dimensions={0}, use_global_device_ids=true | all-gather | bytes 294912 | tf_op jit(solution)/shard_map/all_gather | solution.py:94
  210.5 120.3 %while.61 = (s32[]{:T(128)}, f32[8,2,8,64,128]{4,3,2,1,0:T(8,128)}, f32[8,2,8,64,192]{4,3,2,1,0:T(8,128)}, f32[8,2,8,64]{3,2,1,0:T(8,128)S(1)}, s32[]{:T(128)}, /*index=5*/f32[]{:T(128)}, f32[]{:T(128)}, s32[]{:T(128)}, s32[]{}) while((s32[]{:T(128)}, f32[8,2,8,64,128]{4,3,2,1,0:T(8,128)}, f32[8,2,8,64,192]{4,3,2,1,0:T(8,128)}, ...), condition=%wide.region_7.8_spmd, body=%wide.region_6.7_spmd.sunk | while | flops 604248064 | bytes 18950932 | solution.py:109
  333.6 13.1 %psum.63 = f32[8]{0:T(128)S(1)} all-reduce(f32[8]{0:T(128)S(1)} %get-tuple-element.141), channel_id=1, replica_groups=mesh['freq'=4,'trace'=8] {'freq'}, use_global_device_ids=true, to_apply=%region_5.6 | all-reduce | flops 8 | bytes 64 | tf_op jit(solution)/shard_map/psum | solution.py:103
  346.6 37.2 %all-reduce.5 = (f32[8]{0:T(128)S(1)}, f32[8]{0:T(128)S(1)}) all-reduce(f32[8]{0:T(128)S(1)} %multiply_reduce_fusion.2, f32[8]{0:T(128)S(1)} %get-tuple-element.140), channel_id=1, replica_groups=mesh['freq'=4,'trace'=8] {'freq','trace'}, use_global_device_ids=true, to_apply=%region_9.10 | all-reduce | flops 16 | bytes 128 | tf_op jit(solution)/shard_map/psum | solution.py:113
  383.9 6.0 fusion.47
  389.9 140.6 %while.62 = (s32[]{:T(128)}, f32[8,2,8,64]{3,2,1,0:T(8,128)S(1)}, f32[8,2,8,64,128]{4,3,2,1,0:T(8,128)}, f32[8,2,8,64,192]{4,3,2,1,0:T(8,128)}, s32[]{:T(128)}, /*index=5*/s32[]{:T(128)}, s32[]{}, f32[]{:T(128)}) while((s32[]{:T(128)}, f32[8,2,8,64]{3,2,1,0:T(8,128)S(1)}, f32[8,2,8,64,128]{4,3,2,1,0:T(8,128)}, ...), condition=%wide.region_14.15_spmd, body=%wide.region_12.14_spmd.sunk | while | flops 606346240 | bytes 22103216 | solution.py:99
  402.9 4.2 reshape.134
  455.6 4.2 reshape.134
  473.2 4.2 reshape.134
  508.4 4.2 reshape.134
  530.5 10.6 all-gather.1
  541.4 11.2 %psum.66 = f32[8]{0:T(128)S(1)} all-reduce(f32[8]{0:T(128)S(1)} %multiply_reduce_fusion.5), channel_id=1, replica_groups=mesh['freq'=4,'trace'=8] {'freq'}, use_global_device_ids=true, to_apply=%region_17.18 | all-reduce | flops 8 | bytes 64 | tf_op jit(solution)/shard_map/psum | solution.py:103
  558.3 120.0 %while.63 = (s32[]{:T(128)}, f32[8,2,8,64,128]{4,3,2,1,0:T(8,128)}, f32[8,2,8,64,192]{4,3,2,1,0:T(8,128)}, f32[8,2,8,64]{3,2,1,0:T(8,128)S(1)}, s32[]{:T(128)}, /*index=5*/f32[]{:T(128)}, f32[]{:T(128)}, s32[]{:T(128)}, s32[]{}) while((s32[]{:T(128)}, f32[8,2,8,64,128]{4,3,2,1,0:T(8,128)}, f32[8,2,8,64,192]{4,3,2,1,0:T(8,128)}, ...), condition=%wide.region_19.20_spmd, body=%wide.region_18.19_spmd.sunk | while | flops 604248064 | bytes 18950932 | solution.py:109
  681.2 40.5 %all-reduce.4 = (f32[8]{0:T(128)S(1)}, f32[8]{0:T(128)S(1)}) all-reduce(f32[8]{0:T(128)S(1)} %multiply_reduce_fusion.1, f32[8]{0:T(128)S(1)} %multiply_reduce_fusion.4), channel_id=1, replica_groups=mesh['freq'=4,'trace'=8] {'freq','trace'}, use_global_device_ids=true, to_apply=%region_21.22 | all-reduce | flops 16 | bytes 128 | tf_op jit(solution)/shard_map/psum | solution.py:113
  721.7 6.0 fusion.46
  727.7 140.6 %while.64 = (s32[]{:T(128)}, f32[8,2,8,64]{3,2,1,0:T(8,128)S(1)}, f32[8,2,8,64,128]{4,3,2,1,0:T(8,128)}, f32[8,2,8,64,192]{4,3,2,1,0:T(8,128)}, s32[]{:T(128)}, /*index=5*/s32[]{:T(128)}, s32[]{}, f32[]{:T(128)}) while((s32[]{:T(128)}, f32[8,2,8,64]{3,2,1,0:T(8,128)S(1)}, f32[8,2,8,64,128]{4,3,2,1,0:T(8,128)}, ...), condition=%wide.region_26.27_spmd, body=%wide.region_24.26_spmd.sunk | while | flops 606346240 | bytes 22103216 | solution.py:99
  740.7 4.2 reshape.135
  868.3 10.6 all-gather.2
  879.2 9.9 psum.69
  895.6 119.7 %while.65 = (s32[]{:T(128)}, f32[8,2,8,64,128]{4,3,2,1,0:T(8,128)}, f32[8,2,8,64,192]{4,3,2,1,0:T(8,128)}, f32[8,2,8,64]{3,2,1,0:T(8,128)S(1)}, s32[]{:T(128)}, /*index=5*/f32[]{:T(128)}, f32[]{:T(128)}, s32[]{:T(128)}, s32[]{}) while((s32[]{:T(128)}, f32[8,2,8,64,128]{4,3,2,1,0:T(8,128)}, f32[8,2,8,64,192]{4,3,2,1,0:T(8,128)}, ...), condition=%wide.region_31.32_spmd, body=%wide.region_30.31_spmd.sunk | while | flops 604248064 | bytes 18950932 | solution.py:109
  1018.1 40.3 %all-reduce.3 = (f32[8]{0:T(128)S(1)}, f32[8]{0:T(128)S(1)}) all-reduce(f32[8]{0:T(128)S(1)} %multiply_reduce_fusion, f32[8]{0:T(128)S(1)} %fusion.51), channel_id=1, replica_groups=mesh['freq'=4,'trace'=8] {'freq','trace'}, use_global_device_ids=true, to_apply=%region_33.34 | all-reduce | flops 16 | bytes 128 | tf_op jit(solution)/shard_map/psum | solution.py:113
  1059.2 6.1 fusion.45
  (756 shorter events, 775.4 us)
Async XLA Ops:
  11.4 6.8 collective-permute-start
  16.7 6.7 collective-permute-start.1
  203.2 130.2 %collective-permute-start.2 = (f32[8,2,1,64]{3,2,1,0:T(1,128)S(1)}, f32[8,2,1,64]{3,2,1,0:T(1,128)S(1)}, u32[]{:S(2)}, u32[]{:S(2)}) collective-permute-start(f32[8,2,1,64]{3,2,1,0:T(1,128)S(1)} %get-tuple-element.214), channel_id=1, source_target_pairs={{0,8},{8,16},{16,24},{1,9},{9,17},{17,25},{2,10},{10,18},{18,26},{... | collective-permute-start | bytes 12296 | tf_op jit(solution)/shard_map/ppermute | solution.py:18
  206.7 126.7 %collective-permute-start.3 = (f32[8,2,1,64]{3,2,1,0:T(1,128)S(1)}, f32[8,2,1,64]{3,2,1,0:T(1,128)S(1)}, u32[]{:S(2)}, u32[]{:S(2)}) collective-permute-start(f32[8,2,1,64]{3,2,1,0:T(1,128)S(1)} %get-tuple-element.215), channel_id=1, source_target_pairs={{8,0},{16,8},{24,16},{9,1},{17,9},{25,17},{10,2},{18,10},{26,18},{... | collective-permute-start | bytes 12296 | tf_op jit(solution)/shard_map/ppermute | solution.py:19
  552.7 128.3 %collective-permute-start.4 = (f32[8,2,1,64]{3,2,1,0:T(1,128)S(1)}, f32[8,2,1,64]{3,2,1,0:T(1,128)S(1)}, u32[]{:S(2)}, u32[]{:S(2)}) collective-permute-start(f32[8,2,1,64]{3,2,1,0:T(1,128)S(1)} %get-tuple-element.212), channel_id=1, source_target_pairs={{0,8},{8,16},{16,24},{1,9},{9,17},{17,25},{2,10},{10,18},{18,26},{... | collective-permute-start | bytes 12296 | tf_op jit(solution)/shard_map/ppermute | solution.py:18
  554.3 126.7 %collective-permute-start.5 = (f32[8,2,1,64]{3,2,1,0:T(1,128)S(1)}, f32[8,2,1,64]{3,2,1,0:T(1,128)S(1)}, u32[]{:S(2)}, u32[]{:S(2)}) collective-permute-start(f32[8,2,1,64]{3,2,1,0:T(1,128)S(1)} %get-tuple-element.213), channel_id=1, source_target_pairs={{8,0},{16,8},{24,16},{9,1},{17,9},{25,17},{10,2},{18,10},{26,18},{... | collective-permute-start | bytes 12296 | tf_op jit(solution)/shard_map/ppermute | solution.py:19
  889.2 128.8 %collective-permute-start.6 = (f32[8,2,1,64]{3,2,1,0:T(1,128)S(1)}, f32[8,2,1,64]{3,2,1,0:T(1,128)S(1)}, u32[]{:S(2)}, u32[]{:S(2)}) collective-permute-start(f32[8,2,1,64]{3,2,1,0:T(1,128)S(1)} %get-tuple-element.210), channel_id=1, source_target_pairs={{0,8},{8,16},{16,24},{1,9},{9,17},{17,25},{2,10},{10,18},{18,26},{... | collective-permute-start | bytes 12296 | tf_op jit(solution)/shard_map/ppermute | solution.py:18
  891.6 126.4 %collective-permute-start.7 = (f32[8,2,1,64]{3,2,1,0:T(1,128)S(1)}, f32[8,2,1,64]{3,2,1,0:T(1,128)S(1)}, u32[]{:S(2)}, u32[]{:S(2)}) collective-permute-start(f32[8,2,1,64]{3,2,1,0:T(1,128)S(1)} %get-tuple-element.211), channel_id=1, source_target_pairs={{8,0},{16,8},{24,16},{9,1},{17,9},{25,17},{10,2},{18,10},{26,18},{... | collective-permute-start | bytes 12296 | tf_op jit(solution)/shard_map/ppermute | solution.py:19
